TPU v7x, 32 devices: a whole 2x2x4 slice. The times are simulated.
32 devices in a mesh: dp: 8 (over y, x, core), seq: 4 (over z).
Axes of the slice: x: 2, y: 2, z: 4, core: 2. Of those that a mesh axis runs over, the one named last changes fastest.
Arguments:
- img_q_raw: bfloat16 [8, 512, 1536], P('dp', 'seq'), may hold values from -12 to 12
- img_k_raw: bfloat16 [8, 512, 1536], P('dp', 'seq'), may hold values from -6 to 6
- img_v: bfloat16 [8, 512, 1536], P('dp', 'seq'), may hold values from -6 to 6
- img_dout: bfloat16 [8, 512, 1536], P('dp', 'seq'), may hold values from -6 to 6
- txt_q_raw: bfloat16 [8, 64, 1536], P('dp', 'seq'), may hold values from -6 to 6
- txt_k_raw: bfloat16 [8, 64, 1536], P('dp'), may hold values from -6 to 6
- txt_v: bfloat16 [8, 64, 1536], P('dp'), may hold values from -6 to 6
- txt_dout: bfloat16 [8, 64, 1536], P('dp', 'seq'), may hold values from -6 to 6
- q_gain: float32 [128], replicated, may hold values from 0.6 to 3.8
- k_gain: float32 [128], replicated, may hold values from 0.6 to 3.8
Outputs:
- img_dq: bfloat16 [8, 512, 1536], P('dp', 'seq')
- img_dk: bfloat16 [8, 512, 1536], P('dp', 'seq')
- img_dv: bfloat16 [8, 512, 1536], P('dp', 'seq')
- txt_dq: bfloat16 [8, 64, 1536], P('dp', 'seq')
- txt_dk: bfloat16 [8, 64, 1536], P('dp', 'seq')
- txt_dv: bfloat16 [8, 64, 1536], P('dp', 'seq')
- q_gain_grad: float32 [128], replicated
- k_gain_grad: float32 [128], replicated
All inputs are finite; a program needn't handle non-finite values.
Results may differ from a plain program's by a relative error of at most 0.012.
The roundings to bfloat16 on the way count: a program that leaves them out, or rounds other values in their place, can miss the bound.
Values may be sent and summed in bfloat16 or wider, within the bound.
A program may use at most 64 MiB of HBM per device.

v0:
```python
import jax
import jax.numpy as jnp
from jax import lax
from jax.sharding import PartitionSpec as P

HEAD_DIM = 128
epsilon = 1e-06


def normalize(source, norm_gain):
    values = source.astype(jnp.float32)
    inverse = lax.rsqrt(jnp.mean(values * values, axis=-1, keepdims=True) + epsilon)
    return values * inverse * norm_gain


def norm_backward(source, norm_gain, upstream):
    values = source.astype(jnp.float32)
    result_value, pullback = jax.vjp(normalize, values, norm_gain)
    return pullback(upstream)


def group_back(operands):
    query_b, key_b, value_all, dout_blocks = operands
    score_scale = query_b.shape[-1] ** (-0.5)
    scores = (
        jnp.einsum("nqhd,khd->nhqk", query_b, key_b, preferred_element_type=jnp.float32)
        * score_scale
    )
    row_max = jnp.max(scores, axis=-1, keepdims=True)
    shifted = scores - row_max
    log_total = jnp.log(jnp.sum(jnp.exp(shifted), axis=-1, keepdims=True))
    prob_full = jnp.exp(shifted - log_total)
    probs_b = prob_full.astype(jnp.bfloat16)
    output_b = jnp.einsum(
        "nhqk,khd->nqhd", probs_b, value_all, preferred_element_type=jnp.float32
    ).astype(jnp.bfloat16)
    output_b = lax.optimization_barrier(output_b)
    dprob = jnp.einsum("nqhd,khd->nhqk", dout_blocks, value_all, preferred_element_type=jnp.float32)
    row_delta = jnp.sum(dout_blocks.astype(jnp.float32) * output_b.astype(jnp.float32), axis=-1)
    row_delta = jnp.transpose(row_delta, (0, 2, 1))[..., None]
    dscore_b = (prob_full * (dprob - row_delta) * score_scale).astype(jnp.bfloat16)
    dquery = jnp.einsum("nhqk,khd->nqhd", dscore_b, key_b, preferred_element_type=jnp.float32)
    key_terms = jnp.einsum("nhqk,nqhd->nkhd", dscore_b, query_b, preferred_element_type=jnp.float32)
    value_terms = jnp.einsum(
        "nhqk,nqhd->nkhd", probs_b, dout_blocks, preferred_element_type=jnp.float32
    )
    return (dquery, key_terms, value_terms)


def forward_back(query_b, key_b, value_all, dout_blocks):
    block_count, query_rows, heads_here, feature_count = query_b.shape
    key_rows = key_b.shape[0]
    group_count = heads_here // heads_here

    def split_rows(source):
        return jnp.moveaxis(
            source.reshape(block_count, query_rows, group_count, heads_here, feature_count), 2, 0
        )

    def split_keys(source):
        return jnp.moveaxis(source.reshape(key_rows, group_count, heads_here, feature_count), 1, 0)

    dquery_g, key_g, value_g = lax.map(
        group_back,
        (split_rows(query_b), split_keys(key_b), split_keys(value_all), split_rows(dout_blocks)),
    )
    dquery = jnp.moveaxis(dquery_g, 0, 2).reshape(
        block_count, query_rows, heads_here, feature_count
    )
    key_terms = jnp.moveaxis(key_g, 0, 2).reshape(block_count, key_rows, heads_here, feature_count)
    value_terms = jnp.moveaxis(value_g, 0, 2).reshape(
        block_count, key_rows, heads_here, feature_count
    )
    return (dquery, key_terms, value_terms)


def local(
    img_q_raw, img_k_raw, img_v, img_dout, txt_q_raw, txt_k_raw, txt_v, txt_dout, q_gain, k_gain
):
    seq_count = lax.axis_size("seq")
    my_index = lax.axis_index("seq")
    image_q = img_q_raw[0]
    image_k = img_k_raw[0]
    image_v = img_v[0]
    image_d = img_dout[0]
    text_q = txt_q_raw[0]
    text_k = txt_k_raw[0]
    text_v = txt_v[0]
    text_d = txt_dout[0]
    lane_width = image_q.shape[1]
    head_count = lane_width // HEAD_DIM
    img_rows = image_q.shape[0]
    text_rows = text_q.shape[0]
    text_all = text_k.shape[0]
    image_total = img_rows * seq_count
    exchanged = (
        lax.all_to_all(image_q, "seq", split_axis=1, concat_axis=0, tiled=True),
        lax.all_to_all(image_k, "seq", split_axis=1, concat_axis=0, tiled=True),
        lax.all_to_all(image_v, "seq", split_axis=1, concat_axis=0, tiled=True),
        lax.all_to_all(image_d, "seq", split_axis=1, concat_axis=0, tiled=True),
        lax.all_to_all(text_q, "seq", split_axis=1, concat_axis=0, tiled=True),
        lax.all_to_all(text_d, "seq", split_axis=1, concat_axis=0, tiled=True),
    )
    moved_iq, moved_ik, moved_iv, moved_id, moved_tq, moved_td = exchanged
    local_heads = head_count // seq_count
    head_lanes = local_heads * HEAD_DIM
    key_text = lax.dynamic_slice_in_dim(text_k, my_index * head_lanes, head_lanes, 1)
    value_text = lax.dynamic_slice_in_dim(text_v, my_index * head_lanes, head_lanes, 1)
    query_src = jnp.concatenate(
        [
            moved_iq.reshape(seq_count, img_rows, local_heads, HEAD_DIM),
            moved_tq.reshape(seq_count, text_rows, local_heads, HEAD_DIM),
        ],
        axis=1,
    )
    dout_blocks = jnp.concatenate(
        [
            moved_id.reshape(seq_count, img_rows, local_heads, HEAD_DIM),
            moved_td.reshape(seq_count, text_rows, local_heads, HEAD_DIM),
        ],
        axis=1,
    )
    key_src = jnp.concatenate([moved_ik, key_text], axis=0).reshape(
        image_total + text_all, local_heads, HEAD_DIM
    )
    value_all = jnp.concatenate([moved_iv, value_text], axis=0).reshape(
        image_total + text_all, local_heads, HEAD_DIM
    )
    query_b = normalize(query_src, q_gain).astype(jnp.bfloat16)
    key_b = normalize(key_src, k_gain).astype(jnp.bfloat16)
    dquery, key_f, value_f = forward_back(query_b, key_b, value_all, dout_blocks)
    key_terms = key_f.astype(jnp.bfloat16)
    value_terms = value_f.astype(jnp.bfloat16)
    key_terms, value_terms = lax.optimization_barrier((key_terms, value_terms))
    dkey = jnp.sum(key_terms.astype(jnp.float32), axis=0)
    dvalue = jnp.sum(value_terms.astype(jnp.float32), axis=0)
    dquery_src, dq_gain = norm_backward(query_src, q_gain, dquery)
    dkey_src, dk_gain = norm_backward(key_src, k_gain, dkey)
    dq_b = dquery_src.astype(jnp.bfloat16)
    dk_b = dkey_src.reshape(image_total + text_all, head_lanes).astype(jnp.bfloat16)
    dv_b = dvalue.reshape(image_total + text_all, head_lanes).astype(jnp.bfloat16)
    returned = (
        dq_b[:, :img_rows].reshape(image_total, head_lanes),
        dk_b[:image_total],
        dv_b[:image_total],
        dq_b[:, img_rows:].reshape(text_all, head_lanes),
        dk_b[image_total:],
        dv_b[image_total:],
    )
    grad_iq, grad_ik, grad_iv, grad_tq, grad_tk, grad_tv = (
        lax.all_to_all(returned[0], "seq", split_axis=0, concat_axis=1, tiled=True),
        lax.all_to_all(returned[1], "seq", split_axis=0, concat_axis=1, tiled=True),
        lax.all_to_all(returned[2], "seq", split_axis=0, concat_axis=1, tiled=True),
        lax.all_to_all(returned[3], "seq", split_axis=0, concat_axis=1, tiled=True),
        lax.all_to_all(returned[4], "seq", split_axis=0, concat_axis=1, tiled=True),
        lax.all_to_all(returned[5], "seq", split_axis=0, concat_axis=1, tiled=True),
    )
    gain_q, gain_k = lax.psum((dq_gain, dk_gain), ("dp", "seq"))
    return (
        grad_iq[None],
        grad_ik[None],
        grad_iv[None],
        grad_tq[None],
        grad_tk[None],
        grad_tv[None],
        gain_q,
        gain_k,
    )


def solution(mesh):
    return jax.shard_map(
        local,
        mesh=mesh,
        in_specs=(
            P("dp", "seq", None),
            P("dp", "seq", None),
            P("dp", "seq", None),
            P("dp", "seq", None),
            P("dp", "seq", None),
            P("dp", None, None),
            P("dp", None, None),
            P("dp", "seq", None),
            P(),
            P(),
        ),
        out_specs=(
            P("dp", "seq", None),
            P("dp", "seq", None),
            P("dp", "seq", None),
            P("dp", "seq", None),
            P("dp", "seq", None),
            P("dp", "seq", None),
            P(),
            P(),
        ),
        check_vma=False,
    )
```

profile of v0, /device:TPU:0, one launch (start us, length us, event | category | flops | bytes accessed | tf_op | source)
XLA Modules:
  0.0 206.6 jit_solution(5955745471128264303)
XLA Ops:
  2.2 6.3 %all-to-all-start.2 = ((bf16[16,4,384]{2,0,1:T(8,128)(2,1)}), bf16[16,4,384]{2,0,1:T(8,128)(2,1)S(1)}, u32[]{:S(2)}, u32[]{:S(2)}) async-start(bf16[16,4,384]{2,0,1:T(8,128)(2,1)} %copy.91), calls=%async_computation.2 | async-start | bytes 98304 | tf_op jit(solution)/shard_map/all_to_all | solution.py:101
  9.9 4.3 %all-to-all-done.2 = bf16[16,4,384]{2,0,1:T(8,128)(2,1)S(1)} async-done(((bf16[16,4,384]{2,0,1:T(8,128)(2,1)}), bf16[16,4,384]{2,0,1:T(8,128)(2,1)S(1)}, u32[]{:S(2)}, u32[]{:S(2)}) %all-to-all-start.2) | async-done | bytes 49184 | tf_op jit(solution)/shard_map/all_to_all | solution.py:101
  14.2 3.3 %all-to-all-start.5 = ((bf16[16,4,384]{2,0,1:T(8,128)(2,1)}), bf16[16,4,384]{2,0,1:T(8,128)(2,1)S(1)}, u32[]{:S(2)}, u32[]{:S(2)}) async-start(bf16[16,4,384]{2,0,1:T(8,128)(2,1)} %copy.99), calls=%async_computation.5 | async-start | bytes 98304 | tf_op jit(solution)/shard_map/all_to_all | solution.py:102
  19.4 3.8 %all-to-all-done.5 = bf16[16,4,384]{2,0,1:T(8,128)(2,1)S(1)} async-done(((bf16[16,4,384]{2,0,1:T(8,128)(2,1)}), bf16[16,4,384]{2,0,1:T(8,128)(2,1)S(1)}, u32[]{:S(2)}, u32[]{:S(2)}) %all-to-all-start.5) | async-done | bytes 49184 | tf_op jit(solution)/shard_map/all_to_all | solution.py:102
  23.1 3.5 %all-to-all-start = ((bf16[128,4,384]{0,2,1:T(8,128)(2,1)}), bf16[128,4,384]{0,2,1:T(8,128)(2,1)S(1)}, u32[]{:S(2)}, u32[]{:S(2)}) async-start(bf16[128,4,384]{0,2,1:T(8,128)(2,1)} %bitcast), calls=%async_computation | async-start | bytes 786432 | tf_op jit(solution)/shard_map/all_to_all | solution.py:98
  36.0 3.5 %all-to-all-start.1 = ((bf16[128,4,384]{0,2,1:T(8,128)(2,1)}), bf16[128,4,384]{0,2,1:T(8,128)(2,1)S(1)}, u32[]{:S(2)}, u32[]{:S(2)}) async-start(bf16[128,4,384]{0,2,1:T(8,128)(2,1)} %bitcast.4), calls=%async_computation.1 | async-start | bytes 786432 | tf_op jit(solution)/shard_map/all_to_all | solution.py:97
  40.2 8.6 %all-to-all-done.1 = bf16[128,4,384]{0,2,1:T(8,128)(2,1)S(1)} async-done(((bf16[128,4,384]{0,2,1:T(8,128)(2,1)}), bf16[128,4,384]{0,2,1:T(8,128)(2,1)S(1)}, u32[]{:S(2)}, u32[]{:S(2)}) %all-to-all-start.1) | async-done | bytes 393248 | tf_op jit(solution)/shard_map/all_to_all | solution.py:97
  48.7 3.5 %all-to-all-start.3 = ((bf16[128,4,384]{0,2,1:T(8,128)(2,1)}), bf16[128,4,384]{0,2,1:T(8,128)(2,1)S(1)}, u32[]{:S(2)}, u32[]{:S(2)}) async-start(bf16[128,4,384]{0,2,1:T(8,128)(2,1)} %bitcast.12), calls=%async_computation.3 | async-start | bytes 786432 | tf_op jit(solution)/shard_map/all_to_all | solution.py:99
  54.5 2.9 %fusion.39 = f32[3,576,576]{1,2,0} fusion(bf16[3,128,576]{1,2,0:T(8,128)(2,1)S(1)} %bitcast.111, f32[128]{0:T(128)S(1)} %copy-done.15, f32[576,3]{0,1:T(4,128)S(1)} %fusion.43, bf16[64,3,128]{2,0,1:T(8,128)(2,1)S(1)} %copy.89, bf16[512,3,128]{2,0,1:T(8,128)(2,1)S(1)} %copy.88), kind=kOutput, calls=%fused_computation.57 | convolution fusion | flops 256352256 | bytes 4873472
  57.3 4.2 %all-to-all-done.3 = bf16[128,4,384]{0,2,1:T(8,128)(2,1)S(1)} async-done(((bf16[128,4,384]{0,2,1:T(8,128)(2,1)}), bf16[128,4,384]{0,2,1:T(8,128)(2,1)S(1)}, u32[]{:S(2)}, u32[]{:S(2)}) %all-to-all-start.3) | async-done | bytes 393248 | tf_op jit(solution)/shard_map/all_to_all | solution.py:99
  61.5 3.6 %all-to-all-start.4 = ((bf16[128,4,384]{0,2,1:T(8,128)(2,1)}), bf16[128,4,384]{0,2,1:T(8,128)(2,1)S(1)}, u32[]{:S(2)}, u32[]{:S(2)}) async-start(bf16[128,4,384]{0,2,1:T(8,128)(2,1)} %bitcast.14), calls=%async_computation.4 | async-start | bytes 786432 | tf_op jit(solution)/shard_map/all_to_all | solution.py:100
  65.2 6.4 %bitcast_subtract_fusion = f32[4,3,144,576]{3,2,0,1:T(8,128)} fusion(f32[3,576,4,144]{1,3,2,0:T(8,128)} %bitcast.107), kind=kOutput, calls=%fused_computation.5 | output fusion | flops 2988287 | bytes 7962624 | tf_op jit(solution)/shard_map/while/body/eval_jaxpr/sub | solution.py:30
  72.9 7.0 %fusion.47 = (bf16[4,3,144,576]{3,2,0,1:T(8,128)(2,1)S(1)}, f32[4,3,144,576]{3,2,0,1:T(8,128)}) fusion(f32[4,3,144,576]{3,2,0,1:T(8,128)} %bitcast_subtract_fusion), kind=kOutput, calls=%fused_computation.75 | output fusion | flops 1992959 | bytes 9953280 | tf_op jit(solution)/shard_map/while/body/eval_jaxpr/reduce_sum | solution.py:31
  98.4 4.9 %all-to-all-start.10 = ((bf16[4,16,384]{2,1,0:T(8,128)(2,1)}), bf16[4,16,384]{2,1,0:T(8,128)(2,1)S(1)}, u32[]{:S(2)}, u32[]{:S(2)}) async-start(bf16[4,16,384]{2,1,0:T(8,128)(2,1)} %bitcast.44), calls=%async_computation.10 | async-start | bytes 98304 | tf_op jit(solution)/shard_map/all_to_all | solution.py:155
  109.0 3.5 %all-to-all-start.11 = ((bf16[4,16,384]{2,1,0:T(8,128)(2,1)}), bf16[4,16,384]{2,1,0:T(8,128)(2,1)S(1)}, u32[]{:S(2)}, u32[]{:S(2)}) async-start(bf16[4,16,384]{2,1,0:T(8,128)(2,1)} %all_to_all.177), calls=%async_computation.11 | async-start | bytes 98304 | tf_op jit(solution)/shard_map/all_to_all | solution.py:156
  113.2 5.0 %all-to-all-done.11 = bf16[4,16,384]{2,1,0:T(8,128)(2,1)S(1)} async-done(((bf16[4,16,384]{2,1,0:T(8,128)(2,1)}), bf16[4,16,384]{2,1,0:T(8,128)(2,1)S(1)}, u32[]{:S(2)}, u32[]{:S(2)}) %all-to-all-start.11) | async-done | bytes 49184 | tf_op jit(solution)/shard_map/all_to_all | solution.py:156
  118.2 3.3 %all-to-all-start.9 = ((bf16[4,16,384]{2,1,0:T(8,128)(2,1)}), bf16[4,16,384]{2,1,0:T(8,128)(2,1)S(1)}, u32[]{:S(2)}, u32[]{:S(2)}) async-start(bf16[4,16,384]{2,1,0:T(8,128)(2,1)} %copy_bitcast_fusion), calls=%async_computation.9 | async-start | bytes 98304 | tf_op jit(solution)/shard_map/all_to_all | solution.py:154
  122.4 4.8 %all-to-all-done.9 = bf16[4,16,384]{2,1,0:T(8,128)(2,1)S(1)} async-done(((bf16[4,16,384]{2,1,0:T(8,128)(2,1)}), bf16[4,16,384]{2,1,0:T(8,128)(2,1)S(1)}, u32[]{:S(2)}, u32[]{:S(2)}) %all-to-all-start.9) | async-done | bytes 49184 | tf_op jit(solution)/shard_map/all_to_all | solution.py:154
  127.2 3.5 %all-to-all-start.7 = ((bf16[4,128,384]{2,1,0:T(8,128)(2,1)}), bf16[4,128,384]{2,1,0:T(8,128)(2,1)S(1)}, u32[]{:S(2)}, u32[]{:S(2)}) async-start(bf16[4,128,384]{2,1,0:T(8,128)(2,1)} %bitcast.38), calls=%async_computation.7 | async-start | bytes 786432 | tf_op jit(solution)/shard_map/all_to_all | solution.py:152
  131.8 7.7 %all-to-all-done.7 = bf16[4,128,384]{2,1,0:T(8,128)(2,1)S(1)} async-done(((bf16[4,128,384]{2,1,0:T(8,128)(2,1)}), bf16[4,128,384]{2,1,0:T(8,128)(2,1)S(1)}, u32[]{:S(2)}, u32[]{:S(2)}) %all-to-all-start.7) | async-done | bytes 393248 | tf_op jit(solution)/shard_map/all_to_all | solution.py:152
  139.6 5.6 %all-to-all-start.8 = ((bf16[4,128,384]{1,2,0:T(8,128)(2,1)}), bf16[4,128,384]{1,2,0:T(8,128)(2,1)S(1)}, u32[]{:S(2)}, u32[]{:S(2)}) async-start(bf16[4,128,384]{1,2,0:T(8,128)(2,1)} %copy.115), calls=%async_computation.8 | async-start | bytes 786432 | tf_op jit(solution)/shard_map/all_to_all | solution.py:153
  146.1 11.2 %all-to-all-done.8 = bf16[4,128,384]{1,2,0:T(8,128)(2,1)S(1)} async-done(((bf16[4,128,384]{1,2,0:T(8,128)(2,1)}), bf16[4,128,384]{1,2,0:T(8,128)(2,1)S(1)}, u32[]{:S(2)}, u32[]{:S(2)}) %all-to-all-start.8) | async-done | bytes 393248 | tf_op jit(solution)/shard_map/all_to_all | solution.py:153
  157.4 3.5 %all-to-all-start.6 = ((bf16[4,128,384]{1,2,0:T(8,128)(2,1)}), bf16[4,128,384]{1,2,0:T(8,128)(2,1)S(1)}, u32[]{:S(2)}, u32[]{:S(2)}) async-start(bf16[4,128,384]{1,2,0:T(8,128)(2,1)} %bitcast.27), calls=%async_computation.6 | async-start | bytes 786432 | tf_op jit(solution)/shard_map/all_to_all | solution.py:151
  160.8 40.7 %all-reduce = (f32[128]{0:T(128)}, f32[128]{0:T(128)}) all-reduce(f32[128]{0:T(128)S(1)} %copy-done.20, f32[128]{0:T(128)S(1)} %copy-done.19), channel_id=1, replica_groups=mesh['dp'=8,'seq'=4] {'dp','seq'}, use_global_device_ids=true, to_apply=%region_10.11 | all-reduce | flops 256 | bytes 2048 | tf_op jit(solution)/shard_map/psum | solution.py:158
  (123 shorter events, 51.1 us)
Async XLA Ops:
  0.6 32.1 %copy-start.7 = (bf16[1,128,1536]{2,1,0:T(8,128)(2,1)S(1)}, bf16[1,128,1536]{2,1,0:T(8,128)(2,1)}, u32[]{:S(2)}) copy-start(bf16[1,128,1536]{2,1,0:T(8,128)(2,1)} %param.13) | copy-start | bytes 1179652
  0.6 38.8 %copy-start.15 = (f32[128]{0:T(128)S(1)}, f32[128]{0:T(128)}, u32[]{:S(2)}) copy-start(f32[128]{0:T(128)} %param.19) | copy-start | bytes 1540
  2.2 12.0 %all-to-all-start.2 = ((bf16[16,4,384]{2,0,1:T(8,128)(2,1)}), bf16[16,4,384]{2,0,1:T(8,128)(2,1)S(1)}, u32[]{:S(2)}, u32[]{:S(2)}) async-start(bf16[16,4,384]{2,0,1:T(8,128)(2,1)} %copy.91), calls=%async_computation.2 | async-start | bytes 98304 | tf_op jit(solution)/shard_map/all_to_all | solution.py:101
  14.2 8.9 %all-to-all-start.5 = ((bf16[16,4,384]{2,0,1:T(8,128)(2,1)}), bf16[16,4,384]{2,0,1:T(8,128)(2,1)S(1)}, u32[]{:S(2)}, u32[]{:S(2)}) async-start(bf16[16,4,384]{2,0,1:T(8,128)(2,1)} %copy.99), calls=%async_computation.5 | async-start | bytes 98304 | tf_op jit(solution)/shard_map/all_to_all | solution.py:102
  23.1 12.8 %all-to-all-start = ((bf16[128,4,384]{0,2,1:T(8,128)(2,1)}), bf16[128,4,384]{0,2,1:T(8,128)(2,1)S(1)}, u32[]{:S(2)}, u32[]{:S(2)}) async-start(bf16[128,4,384]{0,2,1:T(8,128)(2,1)} %bitcast), calls=%async_computation | async-start | bytes 786432 | tf_op jit(solution)/shard_map/all_to_all | solution.py:98
  27.5 25.9 %copy-start.17 = (f32[128]{0:T(128)S(1)}, f32[128]{0:T(128)}, u32[]{:S(2)}) copy-start(f32[128]{0:T(128)} %param.18) | copy-start | bytes 1540
  36.0 16.3 %copy-start.3 = (bf16[128,4,384]{0,2,1:T(8,128)(2,1)}, bf16[128,4,384]{0,2,1:T(8,128)(2,1)S(1)}, u32[]{:S(2)}) copy-start(bf16[128,4,384]{0,2,1:T(8,128)(2,1)S(1)} %all-to-all-done) | copy-start | bytes 1179652
  36.0 12.8 %all-to-all-start.1 = ((bf16[128,4,384]{0,2,1:T(8,128)(2,1)}), bf16[128,4,384]{0,2,1:T(8,128)(2,1)S(1)}, u32[]{:S(2)}, u32[]{:S(2)}) async-start(bf16[128,4,384]{0,2,1:T(8,128)(2,1)} %bitcast.4), calls=%async_computation.1 | async-start | bytes 786432 | tf_op jit(solution)/shard_map/all_to_all | solution.py:97
  48.7 12.8 %all-to-all-start.3 = ((bf16[128,4,384]{0,2,1:T(8,128)(2,1)}), bf16[128,4,384]{0,2,1:T(8,128)(2,1)S(1)}, u32[]{:S(2)}, u32[]{:S(2)}) async-start(bf16[128,4,384]{0,2,1:T(8,128)(2,1)} %bitcast.12), calls=%async_computation.3 | async-start | bytes 786432 | tf_op jit(solution)/shard_map/all_to_all | solution.py:99
  53.0 18.6 %copy-start.12 = (f32[4,144,3]{1,0,2:T(4,128)}, f32[4,144,3]{1,0,2:T(4,128)S(1)}, u32[]{:S(2)}) copy-start(f32[4,144,3]{1,0,2:T(4,128)S(1)} %fusion.32) | copy-start | bytes 20740
  53.0 18.6 %copy-start.10 = (f32[4,144,3]{1,0,2:T(4,128)}, f32[4,144,3]{1,0,2:T(4,128)S(1)}, u32[]{:S(2)}) copy-start(f32[4,144,3]{1,0,2:T(4,128)S(1)} %fusion.42) | copy-start | bytes 20740
  53.4 18.2 %copy-start.13 = (f32[576,3]{0,1:T(4,128)}, f32[576,3]{0,1:T(4,128)S(1)}, u32[]{:S(2)}) copy-start(f32[576,3]{0,1:T(4,128)S(1)} %fusion.29) | copy-start | bytes 20740
  61.5 18.4 %all-to-all-start.4 = ((bf16[128,4,384]{0,2,1:T(8,128)(2,1)}), bf16[128,4,384]{0,2,1:T(8,128)(2,1)S(1)}, u32[]{:S(2)}, u32[]{:S(2)}) async-start(bf16[128,4,384]{0,2,1:T(8,128)(2,1)} %bitcast.14), calls=%async_computation.4 | async-start | bytes 786432 | tf_op jit(solution)/shard_map/all_to_all | solution.py:100
  91.6 14.2 %copy-start = (bf16[4,576,3,128]{3,1,2,0:T(8,128)(2,1)S(1)}, bf16[4,576,3,128]{3,1,2,0:T(8,128)(2,1)}, u32[]{:S(2)}) copy-start(bf16[4,576,3,128]{3,1,2,0:T(8,128)(2,1)} %convert_bitcast_fusion) | copy-start | bytes 5308420
  92.8 10.5 %copy-start.14 = (f32[4,144,3]{1,0,2:T(4,128)S(1)}, f32[4,144,3]{1,0,2:T(4,128)}, u32[]{:S(2)}) copy-start(f32[4,144,3]{1,0,2:T(4,128)} %get-tuple-element.63) | copy-start | bytes 20740
  98.4 10.6 %all-to-all-start.10 = ((bf16[4,16,384]{2,1,0:T(8,128)(2,1)}), bf16[4,16,384]{2,1,0:T(8,128)(2,1)S(1)}, u32[]{:S(2)}, u32[]{:S(2)}) async-start(bf16[4,16,384]{2,1,0:T(8,128)(2,1)} %bitcast.44), calls=%async_computation.10 | async-start | bytes 98304 | tf_op jit(solution)/shard_map/all_to_all | solution.py:155
  109.0 9.2 %all-to-all-start.11 = ((bf16[4,16,384]{2,1,0:T(8,128)(2,1)}), bf16[4,16,384]{2,1,0:T(8,128)(2,1)S(1)}, u32[]{:S(2)}, u32[]{:S(2)}) async-start(bf16[4,16,384]{2,1,0:T(8,128)(2,1)} %all_to_all.177), calls=%async_computation.11 | async-start | bytes 98304 | tf_op jit(solution)/shard_map/all_to_all | solution.py:156
  112.5 48.3 %copy-start.19 = (f32[128]{0:T(128)S(1)}, f32[128]{0:T(128)}, u32[]{:S(2)}) copy-start(f32[128]{0:T(128)} %get-tuple-element.60) | copy-start | bytes 1540
  112.5 48.3 %copy-start.20 = (f32[128]{0:T(128)S(1)}, f32[128]{0:T(128)}, u32[]{:S(2)}) copy-start(f32[128]{0:T(128)} %get-tuple-element.62) | copy-start | bytes 1540
  118.2 9.1 %all-to-all-start.9 = ((bf16[4,16,384]{2,1,0:T(8,128)(2,1)}), bf16[4,16,384]{2,1,0:T(8,128)(2,1)S(1)}, u32[]{:S(2)}, u32[]{:S(2)}) async-start(bf16[4,16,384]{2,1,0:T(8,128)(2,1)} %copy_bitcast_fusion), calls=%async_computation.9 | async-start | bytes 98304 | tf_op jit(solution)/shard_map/all_to_all | solution.py:154
  121.5 80.1 %copy-start.9 = (bf16[4,16,384]{2,1,0:T(8,128)(2,1)S(1)}, bf16[4,16,384]{2,1,0:T(8,128)(2,1)}, u32[]{:S(2)}) copy-start(bf16[4,16,384]{2,1,0:T(8,128)(2,1)} %copy-done.8) | copy-start | bytes 147460
  127.2 12.3 %all-to-all-start.7 = ((bf16[4,128,384]{2,1,0:T(8,128)(2,1)}), bf16[4,128,384]{2,1,0:T(8,128)(2,1)S(1)}, u32[]{:S(2)}, u32[]{:S(2)}) async-start(bf16[4,128,384]{2,1,0:T(8,128)(2,1)} %bitcast.38), calls=%async_computation.7 | async-start | bytes 786432 | tf_op jit(solution)/shard_map/all_to_all | solution.py:152
  139.6 17.8 %all-to-all-start.8 = ((bf16[4,128,384]{1,2,0:T(8,128)(2,1)}), bf16[4,128,384]{1,2,0:T(8,128)(2,1)S(1)}, u32[]{:S(2)}, u32[]{:S(2)}) async-start(bf16[4,128,384]{1,2,0:T(8,128)(2,1)} %copy.115), calls=%async_computation.8 | async-start | bytes 786432 | tf_op jit(solution)/shard_map/all_to_all | solution.py:153
  157.4 48.3 %all-to-all-start.6 = ((bf16[4,128,384]{1,2,0:T(8,128)(2,1)}), bf16[4,128,384]{1,2,0:T(8,128)(2,1)S(1)}, u32[]{:S(2)}, u32[]{:S(2)}) async-start(bf16[4,128,384]{1,2,0:T(8,128)(2,1)} %bitcast.27), calls=%async_computation.6 | async-start | bytes 786432 | tf_op jit(solution)/shard_map/all_to_all | solution.py:151
  (11 other events, 27.1 us)
where the time goes:
time: 208 us; the launch traced here: 207 us
  waiting for transfers between devices  53.8 us (26%)
  starting transfers between devices  47.8 us (23%)
  blocking collectives  40.7 us (20%)
  local copies, waits for them, and re-layouts  30.2 us (15%)
  other arithmetic  22.3 us (11%)
  matrix products  10.6 us (5%)
    psum x1, blocking collectives, local(): gain_q, gain_k = lax.psum((dq_gain, dk_gain), ('dp', 'seq'))  40.7 us
    unnamed x53, local copies, waits for them, and re-layouts  11.5 us
    all_to_all x1, waiting for transfers between devices, local(): lax.all_to_all(returned[2], 'seq', split_axis=0, concat_axis=1, tiled=True)  11.2 us
    all_to_all x1, waiting for transfers between devices, local(): lax.all_to_all(image_q, 'seq', split_axis=1, concat_axis=0, tiled=True)  8.56 us
    all_to_all x1, waiting for transfers between devices, local(): lax.all_to_all(returned[1], 'seq', split_axis=0, concat_axis=1, tiled=True)  7.73 us
    reduce_sum x1, other arithmetic, group_back(): log_total = jnp.log(jnp.sum(jnp.exp(shifted), axis=-1, keepdims=True))  7 us
    sub x1, other arithmetic, group_back(): shifted = scores - row_max  6.39 us
    all_to_all x1, starting transfers between devices, local(): lax.all_to_all(text_q, 'seq', split_axis=1, concat_axis=0, tiled=True)  6.35 us
  transfers between devices with their start and end apart: 12, of which 10 were waited for; matrix products, arithmetic and copies ran while one was open for 19% of the time, Pallas kernels for 0%

commit v1 on v0

--- a/solution.py
+++ b/solution.py
@@ -1,3 +1,4 @@
+import functools
 import jax
 import jax.numpy as jnp
 from jax import lax
@@ -5,6 +6,28 @@
 
 HEAD_DIM = 128
 epsilon = 1e-06
+
+
+def trees_drive(array_in, mesh_name, dim_k, dim_i):
+    row_out, front = (lax.psum(1, axis_name=mesh_name), lax.axis_index(mesh_name))
+    fresh = list(array_in.shape)
+    mat_out = array_in.shape[dim_k] // row_out
+    fresh[dim_k] = mat_out
+    now = fresh[dim_i]
+    fresh[dim_i] = now * row_out
+    b_next = jnp.zeros(fresh, array_in.dtype)
+    for dev in range(row_out):
+        field_out = lax.dynamic_slice_in_dim(array_in, (front ^ dev) * mat_out, mat_out, axis=dim_k)
+        if dev:
+            cards = []
+            for u in range(row_out):
+                cards.append((u, u ^ dev))
+            field_out = lax.ppermute(field_out, axis_name=mesh_name, perm=cards)
+        b_next = lax.dynamic_update_slice_in_dim(b_next, field_out, (front ^ dev) * now, axis=dim_i)
+    return b_next
+
+
+group_shelves = functools.partial(trees_drive, mesh_name="seq", dim_k=0, dim_i=1)
 
 
 def normalize(source, norm_gain):
@@ -149,7 +172,7 @@
     )
     grad_iq, grad_ik, grad_iv, grad_tq, grad_tk, grad_tv = (
         lax.all_to_all(returned[0], "seq", split_axis=0, concat_axis=1, tiled=True),
-        lax.all_to_all(returned[1], "seq", split_axis=0, concat_axis=1, tiled=True),
+        group_shelves(returned[1]),
         lax.all_to_all(returned[2], "seq", split_axis=0, concat_axis=1, tiled=True),
         lax.all_to_all(returned[3], "seq", split_axis=0, concat_axis=1, tiled=True),
         lax.all_to_all(returned[4], "seq", split_axis=0, concat_axis=1, tiled=True),

time: 208 us -> 195 us (0.938)
  waiting for transfers between devices: 53.8 us -> 42.3 us
    all_to_all x1 -> x0, waiting for transfers between devices: 7.73 us -> none  [local(): lax.all_to_all(returned[1], 'seq', split_axis=0, concat_axis=1, tiled=True)]
    ppermute x0 -> x3, starting transfers between devices: none -> 4.53 us  [trees_drive(): field_out = lax.ppermute(field_out, axis_name=mesh_name, perm=cards)]
    all_to_all x1 -> x0, starting transfers between devices: 3.46 us -> none  [local(): lax.all_to_all(returned[1], 'seq', split_axis=0, concat_axis=1, tiled=True)]
    all_to_all x1, waiting for transfers between devices: 11.2 us -> 7.81 us  [local(): lax.all_to_all(returned[2], 'seq', split_axis=0, concat_axis=1, tiled=True)]
    all_to_all x1, starting transfers between devices: 5.59 us -> 3.46 us  [local(): lax.all_to_all(returned[2], 'seq', split_axis=0, concat_axis=1, tiled=True)]
    unnamed x53 -> x54, local copies, waits for them, and re-layouts: 11.5 us -> 10.6 us
  transfers between devices with their start and end apart: 12 -> 14, of which waited for: 10 -> 9; matrix products, arithmetic and copies ran while one was open for 19% -> 20% of each run, Pallas kernels for 0% -> 0%
where the time goes in v1:
time: 195 us; the launch traced here: 194 us
  starting transfers between devices  48.7 us (25%)
  waiting for transfers between devices  42.3 us (22%)
  blocking collectives  40 us (21%)
  local copies, waits for them, and re-layouts  28.5 us (15%)
  other arithmetic  22.3 us (11%)
  matrix products  10.6 us (5%)
    psum x1, blocking collectives, local(): gain_q, gain_k = lax.psum((dq_gain, dk_gain), ('dp', 'seq'))  40 us
    unnamed x54, local copies, waits for them, and re-layouts  10.6 us
    all_to_all x1, waiting for transfers between devices, local(): lax.all_to_all(image_q, 'seq', split_axis=1, concat_axis=0, tiled=True)  8.56 us
    all_to_all x1, waiting for transfers between devices, local(): lax.all_to_all(returned[2], 'seq', split_axis=0, concat_axis=1, tiled=True)  7.81 us
    reduce_sum x1, other arithmetic, group_back(): log_total = jnp.log(jnp.sum(jnp.exp(shifted), axis=-1, keepdims=True))  7 us
    sub x1, other arithmetic, group_back(): shifted = scores - row_max  6.39 us
    all_to_all x1, starting transfers between devices, local(): lax.all_to_all(text_q, 'seq', split_axis=1, concat_axis=0, tiled=True)  6.35 us
    all_to_all x1, starting transfers between devices, local(): lax.all_to_all(returned[0], 'seq', split_axis=0, concat_axis=1, tiled=True)  5.39 us
  transfers between devices with their start and end apart: 14, of which 9 were waited for; matrix products, arithmetic and copies ran while one was open for 20% of the time, Pallas kernels for 0%

profile of v1, /device:TPU:0, one launch (start us, length us, event | category | flops | bytes accessed | tf_op | source)
XLA Modules:
  0.0 193.6 jit_solution(8451381525795501040)
XLA Ops:
  2.2 6.3 %all-to-all-start.2 = ((bf16[16,4,384]{2,0,1:T(8,128)(2,1)}), bf16[16,4,384]{2,0,1:T(8,128)(2,1)S(1)}, u32[]{:S(2)}, u32[]{:S(2)}) async-start(bf16[16,4,384]{2,0,1:T(8,128)(2,1)} %copy.127), calls=%async_computation.2 | async-start | bytes 98304 | tf_op jit(solution)/shard_map/all_to_all | solution.py:124
  9.9 4.3 %all-to-all-done.2 = bf16[16,4,384]{2,0,1:T(8,128)(2,1)S(1)} async-done(((bf16[16,4,384]{2,0,1:T(8,128)(2,1)}), bf16[16,4,384]{2,0,1:T(8,128)(2,1)S(1)}, u32[]{:S(2)}, u32[]{:S(2)}) %all-to-all-start.2) | async-done | bytes 49184 | tf_op jit(solution)/shard_map/all_to_all | solution.py:124
  14.2 3.3 %all-to-all-start.5 = ((bf16[16,4,384]{2,0,1:T(8,128)(2,1)}), bf16[16,4,384]{2,0,1:T(8,128)(2,1)S(1)}, u32[]{:S(2)}, u32[]{:S(2)}) async-start(bf16[16,4,384]{2,0,1:T(8,128)(2,1)} %copy.135), calls=%async_computation.5 | async-start | bytes 98304 | tf_op jit(solution)/shard_map/all_to_all | solution.py:125
  19.4 3.8 %all-to-all-done.5 = bf16[16,4,384]{2,0,1:T(8,128)(2,1)S(1)} async-done(((bf16[16,4,384]{2,0,1:T(8,128)(2,1)}), bf16[16,4,384]{2,0,1:T(8,128)(2,1)S(1)}, u32[]{:S(2)}, u32[]{:S(2)}) %all-to-all-start.5) | async-done | bytes 49184 | tf_op jit(solution)/shard_map/all_to_all | solution.py:125
  23.1 3.5 %all-to-all-start = ((bf16[128,4,384]{0,2,1:T(8,128)(2,1)}), bf16[128,4,384]{0,2,1:T(8,128)(2,1)S(1)}, u32[]{:S(2)}, u32[]{:S(2)}) async-start(bf16[128,4,384]{0,2,1:T(8,128)(2,1)} %bitcast), calls=%async_computation | async-start | bytes 786432 | tf_op jit(solution)/shard_map/all_to_all | solution.py:121
  36.0 3.5 %all-to-all-start.1 = ((bf16[128,4,384]{0,2,1:T(8,128)(2,1)}), bf16[128,4,384]{0,2,1:T(8,128)(2,1)S(1)}, u32[]{:S(2)}, u32[]{:S(2)}) async-start(bf16[128,4,384]{0,2,1:T(8,128)(2,1)} %bitcast.4), calls=%async_computation.1 | async-start | bytes 786432 | tf_op jit(solution)/shard_map/all_to_all | solution.py:120
  40.2 8.6 %all-to-all-done.1 = bf16[128,4,384]{0,2,1:T(8,128)(2,1)S(1)} async-done(((bf16[128,4,384]{0,2,1:T(8,128)(2,1)}), bf16[128,4,384]{0,2,1:T(8,128)(2,1)S(1)}, u32[]{:S(2)}, u32[]{:S(2)}) %all-to-all-start.1) | async-done | bytes 393248 | tf_op jit(solution)/shard_map/all_to_all | solution.py:120
  48.7 3.5 %all-to-all-start.3 = ((bf16[128,4,384]{0,2,1:T(8,128)(2,1)}), bf16[128,4,384]{0,2,1:T(8,128)(2,1)S(1)}, u32[]{:S(2)}, u32[]{:S(2)}) async-start(bf16[128,4,384]{0,2,1:T(8,128)(2,1)} %bitcast.12), calls=%async_computation.3 | async-start | bytes 786432 | tf_op jit(solution)/shard_map/all_to_all | solution.py:122
  54.5 2.9 %fusion.39 = f32[3,576,576]{1,2,0} fusion(bf16[3,128,576]{1,2,0:T(8,128)(2,1)S(1)} %bitcast.117, f32[128]{0:T(128)S(1)} %copy-done.16, f32[576,3]{0,1:T(4,128)S(1)} %fusion.43, bf16[64,3,128]{2,0,1:T(8,128)(2,1)S(1)} %copy.125, bf16[512,3,128]{2,0,1:T(8,128)(2,1)S(1)} %copy.124), kind=kOutput, calls=%fused_computation.58 | convolution fusion | flops 256352256 | bytes 4873472
  57.4 4.1 %all-to-all-done.3 = bf16[128,4,384]{0,2,1:T(8,128)(2,1)S(1)} async-done(((bf16[128,4,384]{0,2,1:T(8,128)(2,1)}), bf16[128,4,384]{0,2,1:T(8,128)(2,1)S(1)}, u32[]{:S(2)}, u32[]{:S(2)}) %all-to-all-start.3) | async-done | bytes 393248 | tf_op jit(solution)/shard_map/all_to_all | solution.py:122
  61.5 3.6 %all-to-all-start.4 = ((bf16[128,4,384]{0,2,1:T(8,128)(2,1)}), bf16[128,4,384]{0,2,1:T(8,128)(2,1)S(1)}, u32[]{:S(2)}, u32[]{:S(2)}) async-start(bf16[128,4,384]{0,2,1:T(8,128)(2,1)} %bitcast.14), calls=%async_computation.4 | async-start | bytes 786432 | tf_op jit(solution)/shard_map/all_to_all | solution.py:123
  65.2 6.4 %bitcast_subtract_fusion = f32[4,3,144,576]{3,2,0,1:T(8,128)} fusion(f32[3,576,4,144]{1,3,2,0:T(8,128)} %bitcast.113), kind=kOutput, calls=%fused_computation.5 | output fusion | flops 2988287 | bytes 7962624 | tf_op jit(solution)/shard_map/while/body/eval_jaxpr/sub | solution.py:53
  73.0 7.0 %fusion.47 = (bf16[4,3,144,576]{3,2,0,1:T(8,128)(2,1)S(1)}, f32[4,3,144,576]{3,2,0,1:T(8,128)}) fusion(f32[4,3,144,576]{3,2,0,1:T(8,128)} %bitcast_subtract_fusion), kind=kOutput, calls=%fused_computation.84 | output fusion | flops 1992959 | bytes 9953280 | tf_op jit(solution)/shard_map/while/body/eval_jaxpr/reduce_sum | solution.py:54
  82.0 2.5 %convert_bitcast_fusion = bf16[4,576,3,128]{3,1,2,0:T(8,128)(2,1)} fusion(bf16[4,3,144,576]{3,2,0,1:T(8,128)(2,1)S(1)} %get-tuple-element.78, bf16[4,16,3,128]{3,1,0,2:T(8,128)(2,1)S(1)} %copy_bitcast_fusion.2, bf16[4,128,3,128]{3,1,0,2:T(8,128)(2,1)S(1)} %copy.136), kind=kOutput, calls=%fused_computation.17 | convolution fusion | flops 256573440 | bytes 4202496 | tf_op jit(solution)/shard_map/while/body/eval_jaxpr/nhqk,nqhd->nkhd/dot_general | solution.py:67
  88.8 2.5 %fusion.26 = (f32[128]{0:T(128)}, f32[4,144,3]{1,0,2:T(4,128)}, f32[4,144,3,128]{3,1,0,2:T(8,128)}) fusion(f32[4,144,3]{1,0,2:T(4,128)S(1)} %copy-done.12, bf16[4,16,3,128]{3,1,0,2:T(8,128)(2,1)S(1)} %copy_bitcast_fusion.3, bf16[4,128,3,128]{3,1,0,2:T(8,128)(2,1)S(1)} %copy.128, f32[128]{0:T(128)S(1)} %copy-done.19, ...), kind=kOutput, calls=%fused_computation.40 | convolution fusion | flops 258562240 | bytes 3782400 | tf_op jit(solution)/shard_map/while/body/eval_jaxpr/nhqk,khd->nqhd/dot_general | solution.py:65
  98.1 4.9 %all-to-all-start.9 = ((bf16[4,16,384]{2,1,0:T(8,128)(2,1)}), bf16[4,16,384]{2,1,0:T(8,128)(2,1)S(1)}, u32[]{:S(2)}, u32[]{:S(2)}) async-start(bf16[4,16,384]{2,1,0:T(8,128)(2,1)} %bitcast.44), calls=%async_computation.9 | async-start | bytes 98304 | tf_op jit(solution)/shard_map/all_to_all | solution.py:178
  108.7 3.3 %all-to-all-start.10 = ((bf16[4,16,384]{2,1,0:T(8,128)(2,1)}), bf16[4,16,384]{2,1,0:T(8,128)(2,1)S(1)}, u32[]{:S(2)}, u32[]{:S(2)}) async-start(bf16[4,16,384]{2,1,0:T(8,128)(2,1)} %all_to_all.162), calls=%async_computation.10 | async-start | bytes 98304 | tf_op jit(solution)/shard_map/all_to_all | solution.py:179
  112.6 5.0 %all-to-all-done.10 = bf16[4,16,384]{2,1,0:T(8,128)(2,1)S(1)} async-done(((bf16[4,16,384]{2,1,0:T(8,128)(2,1)}), bf16[4,16,384]{2,1,0:T(8,128)(2,1)S(1)}, u32[]{:S(2)}, u32[]{:S(2)}) %all-to-all-start.10) | async-done | bytes 49184 | tf_op jit(solution)/shard_map/all_to_all | solution.py:179
  117.7 3.5 %all-to-all-start.8 = ((bf16[4,16,384]{2,1,0:T(8,128)(2,1)}), bf16[4,16,384]{2,1,0:T(8,128)(2,1)S(1)}, u32[]{:S(2)}, u32[]{:S(2)}) async-start(bf16[4,16,384]{2,1,0:T(8,128)(2,1)} %copy_bitcast_fusion.1), calls=%async_computation.8 | async-start | bytes 98304 | tf_op jit(solution)/shard_map/all_to_all | solution.py:177
  122.3 4.4 %all-to-all-done.8 = bf16[4,16,384]{2,1,0:T(8,128)(2,1)S(1)} async-done(((bf16[4,16,384]{2,1,0:T(8,128)(2,1)}), bf16[4,16,384]{2,1,0:T(8,128)(2,1)S(1)}, u32[]{:S(2)}, u32[]{:S(2)}) %all-to-all-start.8) | async-done | bytes 49184 | tf_op jit(solution)/shard_map/all_to_all | solution.py:177
  126.7 3.5 %all-to-all-start.7 = ((bf16[4,128,384]{1,2,0:T(8,128)(2,1)}), bf16[4,128,384]{1,2,0:T(8,128)(2,1)S(1)}, u32[]{:S(2)}, u32[]{:S(2)}) async-start(bf16[4,128,384]{1,2,0:T(8,128)(2,1)} %copy.152), calls=%async_computation.7 | async-start | bytes 786432 | tf_op jit(solution)/shard_map/all_to_all | solution.py:176
  131.2 7.8 %all-to-all-done.7 = bf16[4,128,384]{1,2,0:T(8,128)(2,1)S(1)} async-done(((bf16[4,128,384]{1,2,0:T(8,128)(2,1)}), bf16[4,128,384]{1,2,0:T(8,128)(2,1)S(1)}, u32[]{:S(2)}, u32[]{:S(2)}) %all-to-all-start.7) | async-done | bytes 393248 | tf_op jit(solution)/shard_map/all_to_all | solution.py:176
  139.0 5.4 %all-to-all-start.6 = ((bf16[4,128,384]{1,2,0:T(8,128)(2,1)}), bf16[4,128,384]{1,2,0:T(8,128)(2,1)S(1)}, u32[]{:S(2)}, u32[]{:S(2)}) async-start(bf16[4,128,384]{1,2,0:T(8,128)(2,1)} %bitcast.27), calls=%async_computation.6 | async-start | bytes 786432 | tf_op jit(solution)/shard_map/all_to_all | solution.py:174
  149.2 40.0 %all-reduce = (f32[128]{0:T(128)}, f32[128]{0:T(128)}) all-reduce(f32[128]{0:T(128)S(1)} %copy-done.21, f32[128]{0:T(128)S(1)} %copy-done.20), channel_id=1, replica_groups=mesh['dp'=8,'seq'=4] {'dp','seq'}, use_global_device_ids=true, to_apply=%region_10.11 | all-reduce | flops 256 | bytes 2048 | tf_op jit(solution)/shard_map/psum | solution.py:181
  (135 shorter events, 48.9 us)
Async XLA Ops:
  0.6 32.1 %copy-start.7 = (bf16[1,128,1536]{2,1,0:T(8,128)(2,1)S(1)}, bf16[1,128,1536]{2,1,0:T(8,128)(2,1)}, u32[]{:S(2)}) copy-start(bf16[1,128,1536]{2,1,0:T(8,128)(2,1)} %param.13) | copy-start | bytes 1179652
  0.6 38.8 %copy-start.16 = (f32[128]{0:T(128)S(1)}, f32[128]{0:T(128)}, u32[]{:S(2)}) copy-start(f32[128]{0:T(128)} %param.19) | copy-start | bytes 1540
  2.2 12.0 %all-to-all-start.2 = ((bf16[16,4,384]{2,0,1:T(8,128)(2,1)}), bf16[16,4,384]{2,0,1:T(8,128)(2,1)S(1)}, u32[]{:S(2)}, u32[]{:S(2)}) async-start(bf16[16,4,384]{2,0,1:T(8,128)(2,1)} %copy.127), calls=%async_computation.2 | async-start | bytes 98304 | tf_op jit(solution)/shard_map/all_to_all | solution.py:124
  14.2 8.9 %all-to-all-start.5 = ((bf16[16,4,384]{2,0,1:T(8,128)(2,1)}), bf16[16,4,384]{2,0,1:T(8,128)(2,1)S(1)}, u32[]{:S(2)}, u32[]{:S(2)}) async-start(bf16[16,4,384]{2,0,1:T(8,128)(2,1)} %copy.135), calls=%async_computation.5 | async-start | bytes 98304 | tf_op jit(solution)/shard_map/all_to_all | solution.py:125
  23.1 12.8 %all-to-all-start = ((bf16[128,4,384]{0,2,1:T(8,128)(2,1)}), bf16[128,4,384]{0,2,1:T(8,128)(2,1)S(1)}, u32[]{:S(2)}, u32[]{:S(2)}) async-start(bf16[128,4,384]{0,2,1:T(8,128)(2,1)} %bitcast), calls=%async_computation | async-start | bytes 786432 | tf_op jit(solution)/shard_map/all_to_all | solution.py:121
  27.5 25.9 %copy-start.18 = (f32[128]{0:T(128)S(1)}, f32[128]{0:T(128)}, u32[]{:S(2)}) copy-start(f32[128]{0:T(128)} %param.18) | copy-start | bytes 1540
  36.0 16.3 %copy-start.3 = (bf16[128,4,384]{0,2,1:T(8,128)(2,1)}, bf16[128,4,384]{0,2,1:T(8,128)(2,1)S(1)}, u32[]{:S(2)}) copy-start(bf16[128,4,384]{0,2,1:T(8,128)(2,1)S(1)} %all-to-all-done) | copy-start | bytes 1179652
  36.0 12.8 %all-to-all-start.1 = ((bf16[128,4,384]{0,2,1:T(8,128)(2,1)}), bf16[128,4,384]{0,2,1:T(8,128)(2,1)S(1)}, u32[]{:S(2)}, u32[]{:S(2)}) async-start(bf16[128,4,384]{0,2,1:T(8,128)(2,1)} %bitcast.4), calls=%async_computation.1 | async-start | bytes 786432 | tf_op jit(solution)/shard_map/all_to_all | solution.py:120
  48.7 12.8 %all-to-all-start.3 = ((bf16[128,4,384]{0,2,1:T(8,128)(2,1)}), bf16[128,4,384]{0,2,1:T(8,128)(2,1)S(1)}, u32[]{:S(2)}, u32[]{:S(2)}) async-start(bf16[128,4,384]{0,2,1:T(8,128)(2,1)} %bitcast.12), calls=%async_computation.3 | async-start | bytes 786432 | tf_op jit(solution)/shard_map/all_to_all | solution.py:122
  53.0 18.6 %copy-start.13 = (f32[4,144,3]{1,0,2:T(4,128)}, f32[4,144,3]{1,0,2:T(4,128)S(1)}, u32[]{:S(2)}) copy-start(f32[4,144,3]{1,0,2:T(4,128)S(1)} %fusion.32) | copy-start | bytes 20740
  53.0 18.6 %copy-start.11 = (f32[4,144,3]{1,0,2:T(4,128)}, f32[4,144,3]{1,0,2:T(4,128)S(1)}, u32[]{:S(2)}) copy-start(f32[4,144,3]{1,0,2:T(4,128)S(1)} %fusion.42) | copy-start | bytes 20740
  53.4 18.2 %copy-start.14 = (f32[576,3]{0,1:T(4,128)}, f32[576,3]{0,1:T(4,128)S(1)}, u32[]{:S(2)}) copy-start(f32[576,3]{0,1:T(4,128)S(1)} %fusion.29) | copy-start | bytes 20740
  61.5 18.5 %all-to-all-start.4 = ((bf16[128,4,384]{0,2,1:T(8,128)(2,1)}), bf16[128,4,384]{0,2,1:T(8,128)(2,1)S(1)}, u32[]{:S(2)}, u32[]{:S(2)}) async-start(bf16[128,4,384]{0,2,1:T(8,128)(2,1)} %bitcast.14), calls=%async_computation.4 | async-start | bytes 786432 | tf_op jit(solution)/shard_map/all_to_all | solution.py:123
  98.1 10.6 %all-to-all-start.9 = ((bf16[4,16,384]{2,1,0:T(8,128)(2,1)}), bf16[4,16,384]{2,1,0:T(8,128)(2,1)S(1)}, u32[]{:S(2)}, u32[]{:S(2)}) async-start(bf16[4,16,384]{2,1,0:T(8,128)(2,1)} %bitcast.44), calls=%async_computation.9 | async-start | bytes 98304 | tf_op jit(solution)/shard_map/all_to_all | solution.py:178
  108.7 8.9 %all-to-all-start.10 = ((bf16[4,16,384]{2,1,0:T(8,128)(2,1)}), bf16[4,16,384]{2,1,0:T(8,128)(2,1)S(1)}, u32[]{:S(2)}, u32[]{:S(2)}) async-start(bf16[4,16,384]{2,1,0:T(8,128)(2,1)} %all_to_all.162), calls=%async_computation.10 | async-start | bytes 98304 | tf_op jit(solution)/shard_map/all_to_all | solution.py:179
  112.6 36.6 %copy-start.20 = (f32[128]{0:T(128)S(1)}, f32[128]{0:T(128)}, u32[]{:S(2)}) copy-start(f32[128]{0:T(128)} %get-tuple-element.68) | copy-start | bytes 1540
  112.6 36.6 %copy-start.21 = (f32[128]{0:T(128)S(1)}, f32[128]{0:T(128)}, u32[]{:S(2)}) copy-start(f32[128]{0:T(128)} %get-tuple-element.70) | copy-start | bytes 1540
  117.7 9.1 %all-to-all-start.8 = ((bf16[4,16,384]{2,1,0:T(8,128)(2,1)}), bf16[4,16,384]{2,1,0:T(8,128)(2,1)S(1)}, u32[]{:S(2)}, u32[]{:S(2)}) async-start(bf16[4,16,384]{2,1,0:T(8,128)(2,1)} %copy_bitcast_fusion.1), calls=%async_computation.8 | async-start | bytes 98304 | tf_op jit(solution)/shard_map/all_to_all | solution.py:177
  121.2 68.1 %copy-start.10 = (bf16[4,16,384]{2,1,0:T(8,128)(2,1)S(1)}, bf16[4,16,384]{2,1,0:T(8,128)(2,1)}, u32[]{:S(2)}) copy-start(bf16[4,16,384]{2,1,0:T(8,128)(2,1)} %copy-done.9) | copy-start | bytes 147460
  126.7 12.3 %all-to-all-start.7 = ((bf16[4,128,384]{1,2,0:T(8,128)(2,1)}), bf16[4,128,384]{1,2,0:T(8,128)(2,1)S(1)}, u32[]{:S(2)}, u32[]{:S(2)}) async-start(bf16[4,128,384]{1,2,0:T(8,128)(2,1)} %copy.152), calls=%async_computation.7 | async-start | bytes 786432 | tf_op jit(solution)/shard_map/all_to_all | solution.py:176
  139.0 53.7 %all-to-all-start.6 = ((bf16[4,128,384]{1,2,0:T(8,128)(2,1)}), bf16[4,128,384]{1,2,0:T(8,128)(2,1)S(1)}, u32[]{:S(2)}, u32[]{:S(2)}) async-start(bf16[4,128,384]{1,2,0:T(8,128)(2,1)} %bitcast.27), calls=%async_computation.6 | async-start | bytes 786432 | tf_op jit(solution)/shard_map/all_to_all | solution.py:174
  144.6 46.6 %collective-permute-start = (bf16[128,384]{0,1:T(8,128)(2,1)S(1)}, bf16[128,384]{0,1:T(8,128)(2,1)S(1)}, u32[]{:S(2)}, u32[]{:S(2)}) collective-permute-start(bf16[128,384]{0,1:T(8,128)(2,1)S(1)} %get-tuple-element.76), channel_id=1, source_target_pairs={{0,1},{1,0},{2,3},{3,2},{4,5},{5,4},{6,7},{7,6},{8,9},{9,8},{10,11... | collective-permute-start | bytes 294920 | tf_op jit(solution)/shard_map/ppermute | solution.py:25
  146.7 44.7 %collective-permute-start.1 = (bf16[128,384]{0,1:T(8,128)(2,1)S(1)}, bf16[128,384]{0,1:T(8,128)(2,1)S(1)}, u32[]{:S(2)}, u32[]{:S(2)}) collective-permute-start(bf16[128,384]{0,1:T(8,128)(2,1)S(1)} %get-tuple-element.75), channel_id=1, source_target_pairs={{0,2},{1,3},{2,0},{3,1},{4,6},{5,7},{6,4},{7,5},{8,10},{9,11},{10,... | collective-permute-start | bytes 294920 | tf_op jit(solution)/shard_map/ppermute | solution.py:25
  149.1 42.5 %collective-permute-start.2 = (bf16[128,384]{0,1:T(8,128)(2,1)S(1)}, bf16[128,384]{0,1:T(8,128)(2,1)S(1)}, u32[]{:S(2)}, u32[]{:S(2)}) collective-permute-start(bf16[128,384]{0,1:T(8,128)(2,1)S(1)} %get-tuple-element.74), channel_id=1, source_target_pairs={{0,3},{1,2},{2,1},{3,0},{4,7},{5,6},{6,5},{7,4},{8,11},{9,10},{10,... | collective-permute-start | bytes 294920 | tf_op jit(solution)/shard_map/ppermute | solution.py:25
  (14 other events, 52.8 us)
